TPU v7x, 32 devices: a whole 2x2x4 slice. The times are simulated.
32 devices in a mesh: dp: 8 (over z, x), tp: 4 (over y, core).
Axes of the slice: x: 2, y: 2, z: 4, core: 2. Of those that a mesh axis runs over, the one named last changes fastest.
Arguments:
- gradients: bfloat16 [8, 4, 5120, 1280], P('dp', None, 'tp'), may hold values from -6 to 6
- right_factor: float32 [4, 1280, 32], replicated, may hold values from -6 to 6
- weights_before: float32 [4, 5120, 1280], P(None, 'tp', 'dp'), may hold values from -0.15625 to 0.15625
- momentum: float32 [4, 5120, 1280], P(None, 'tp', 'dp'), may hold values from -0.3125 to 0.3125
Outputs:
- new_weights: float32 [4, 5120, 1280], P(None, 'tp', 'dp')
- new_basis: float32 [4, 1280, 32], replicated
- new_momentum: float32 [4, 5120, 1280], P(None, 'tp', 'dp')
All inputs are finite; a program needn't handle non-finite values.
Results may differ from a plain program's by a relative error of at most 0.003.
Values sent between devices are 32-bit elements; how exact they have to be, the bound alone decides.
A program may use at most 64 MiB of HBM per device.

v0:
```python
import jax
import jax.numpy as jnp
from jax import lax
from jax.sharding import PartitionSpec as P

RANK = 32


def on_device(gradients, right_factor, weights_before, momentum):
    own_grads = gradients[0]
    part_left = jnp.einsum(
        "liw,lwr->lir",
        own_grads,
        right_factor.astype(jnp.bfloat16),
        preferred_element_type=jnp.float32,
    )
    left = lax.psum(part_left, "dp")
    part_gram = jnp.einsum("lir,lis->lrs", left, left, precision=lax.Precision.HIGHEST)
    small_left = left.astype(jnp.bfloat16)
    gram = lax.psum(part_gram, "tp")
    part_right = jnp.einsum(
        "liw,lir->lwr", own_grads, small_left, preferred_element_type=jnp.float32
    )
    right = lax.psum(part_right, ("dp", "tp"))
    gram = gram + 0.001 * jnp.mean(jnp.diagonal(gram, axis1=1, axis2=2), axis=1)[
        :, None, None
    ] * jnp.eye(RANK, dtype=jnp.float32)
    place = lax.axis_index("dp") * weights_before.shape[2]
    own_right = lax.dynamic_slice_in_dim(right, place, weights_before.shape[2], axis=1)
    root = jnp.linalg.cholesky(gram)
    half = lax.linalg.triangular_solve(
        root, jnp.swapaxes(own_right, 1, 2), left_side=True, lower=True
    )
    mixed = lax.linalg.triangular_solve(root, half, left_side=True, lower=True, transpose_a=True)
    change = jnp.einsum(
        "lir,lrw->liw", left, mixed, precision=lax.Precision.HIGHEST
    ) / lax.axis_size("dp")
    new_momentum = 0.8 * momentum + change
    new_weights = weights_before - 0.05 * new_momentum
    new_basis = right * lax.rsqrt(jnp.mean(right * right, axis=(1, 2), keepdims=True) + 1e-12)
    return (new_weights, new_basis, new_momentum)


def solution(mesh):
    return jax.shard_map(
        on_device,
        mesh=mesh,
        in_specs=(P("dp", None, "tp", None), P(), P(None, "tp", "dp"), P(None, "tp", "dp")),
        out_specs=(P(None, "tp", "dp"), P(), P(None, "tp", "dp")),
        check_vma=False,
    )
```

profile of v0, /device:TPU:0, one launch (start us, length us, event | category | flops | bytes accessed | tf_op | source)
XLA Modules:
  0.0 276.0 jit_solution(18249295536158250338)
XLA Ops:
  7.2 0.0 all-reduce.3.cloned.1.call-start
  7.2 9.6 %fusion.2 = f32[4,1280,32]{1,2,0:T(8,128)} fusion(bf16[1,4,1280,1280]{3,2,1,0:T(8,128)(2,1)} %param.4, f32[4,1280,32]{1,2,0:T(8,128)} %param.5), kind=kOutput, calls=%fused_computation.3 | convolution fusion | flops 419594240 | bytes 14417920 | tf_op jit(solution)/shard_map/liw,lwr->lir/dot_general | solution.py:11
  16.8 0.0 all-reduce.3.cloned.1.call-update
  16.8 0.0 all-reduce.5.cloned.1.call-start
  16.9 0.1 copy.13
  17.0 76.5 %all-reduce.3.cloned.1.call-done = f32[4,1280,32]{1,2,0:T(8,128)} async-done(((f32[4,1280,32]{1,2,0:T(8,128)}), f32[4,1280,32]{1,2,0:T(8,128)}) %all-reduce.3.cloned.1.call-update) | async-done | bytes 655376 | tf_op jit(solution)/shard_map/psum | solution.py:17
  93.4 2.0 fusion.18
  95.5 10.7 %psum.22 = f32[4,32,32]{1,2,0:T(8,128)S(1)} all-reduce(f32[4,32,32]{1,2,0:T(8,128)S(1)} %fusion.18), channel_id=1, replica_groups=mesh['dp'=8,'tp'=4] {'tp'}, use_global_device_ids=true, to_apply=%region_1.0 | all-reduce | flops 4096 | bytes 32768 | tf_op jit(solution)/shard_map/psum | solution.py:20
  106.1 0.5 copy.12
  106.7 0.7 gather_fusion
  107.4 0.1 multiply_add_fusion
  107.5 0.1 copy.14
  107.6 0.1 fusion.15
  107.7 11.7 %custom-call.9 = f32[4,32,32]{2,1,0:T(8,128)S(1)} custom-call(f32[4,32,32]{2,1,0:T(8,128)S(1)} %fusion.15), custom_call_target="Cholesky" | custom-call | tf_op jit(solution)/shard_map/jit(cholesky)/cholesky | solution.py:30
  119.4 8.1 %fusion.5 = f32[4,1280,32]{1,2,0:T(8,128)} fusion(bf16[1,4,1280,1280]{3,2,1,0:T(8,128)(2,1)} %param.4, f32[4,1280,32]{1,2,0:T(8,128)} %all-reduce.3.cloned.1.call-done), kind=kOutput, calls=%fused_computation.8 | convolution fusion | flops 419594240 | bytes 14417920 | tf_op jit(solution)/shard_map/liw,lir->lwr/dot_general | solution.py:21
  127.5 0.0 copy-start
  127.5 0.0 all-reduce.5.cloned.1.call-update
  127.5 0.1 compare_reduce_fusion
  127.7 0.1 select_bitcast_fusion
  127.7 9.8 %custom-call.10 = f32[4,1,32,32]{2,3,1,0:T(8,128)S(1)} custom-call(f32[4,1,32,32]{3,2,1,0:T(8,128)S(1)} %select_bitcast_fusion), custom_call_target="InvertDiagBlocksLowerTriangular" | custom-call | tf_op jit(solution)/shard_map/triangular_solve | solution.py:34
  137.6 119.6 %all-reduce.5.cloned.1.call-done = f32[4,1280,32]{1,2,0:T(8,128)} async-done(((f32[4,1280,32]{1,2,0:T(8,128)}), f32[4,1280,32]{1,2,0:T(8,128)}) %all-reduce.5.cloned.1.call-update) | async-done | bytes 655376 | tf_op jit(solution)/shard_map/psum | solution.py:24
  257.2 1.2 multiply_reduce_fusion
  258.4 1.3 fusion.10
  259.7 0.3 fusion.12
  260.0 2.0 broadcast_multiply_fusion
  262.0 0.0 copy-done
  262.0 7.2 %multiply_subtract_fusion = (f32[4,1280,160]{1,2,0:T(8,128)}, f32[4,1280,160]{1,2,0:T(8,128)}) fusion(f32[4,1280,160]{1,2,0:T(8,128)} %param.6, f32[4,1280,32]{1,2,0:T(8,128)S(1)} %copy-done, f32[4,32,160]{2,1,0:T(8,128)S(1)} %fusion.12, f32[4,1280,160]{1,2,0:T(8,128)} %param.7), kind=kOutput, calls=%fused_computation.7 | convolution fusion | flops 318668800 | bytes 13844480 | tf_op jit(solution)/shard_map/lir,lrw->liw/dot_general | solution.py:35
  (8 shorter events, 0.1 us)
Async XLA Ops:
  7.2 86.3 %all-reduce.3.cloned.1.call-start = ((), (), s32[]{:S(2)}) async-start(), calls=%async_computation | async-start | bytes 1310720 | tf_op jit(solution)/shard_map/psum | solution.py:17
  16.8 240.4 %all-reduce.5.cloned.1.call-start = ((), (), s32[]{:S(2)}) async-start(), calls=%async_computation.1 | async-start | bytes 1310720 | tf_op jit(solution)/shard_map/psum | solution.py:24
  127.5 134.5 %copy-start = (f32[4,1280,32]{1,2,0:T(8,128)S(1)}, f32[4,1280,32]{1,2,0:T(8,128)}, u32[]{:S(2)}) copy-start(f32[4,1280,32]{1,2,0:T(8,128)} %all-reduce.3.cloned.1.call-done) | copy-start | bytes 1966084
Sparse Core Ops, SparseCore 0:
  16.9 76.4 all-reduce.2
  127.6 129.4 all-reduce.4
where the time goes:
time: 276 us
  waiting for transfers between devices  196 us (71%)
  matrix products  28.4 us (10%)
  other arithmetic  25.3 us (9%)
  between operations  14.1 us (5%)
  blocking collectives  10.7 us (4%)
    psum x1, waiting for transfers between devices, on_device(): right = lax.psum(part_right, ('dp', 'tp'))  120 us
    psum x1, waiting for transfers between devices, on_device(): left = lax.psum(part_left, 'dp')  76.5 us
    another operation x4, other arithmetic, on_device(): root = jnp.linalg.cholesky(gram)  11.9 us
    psum x1, blocking collectives, on_device(): gram = lax.psum(part_gram, 'tp')  10.7 us
    another operation x3, other arithmetic, on_device(): lax.linalg.triangular_solve(root, half, left_side=True, lower=True, trans...  9.93 us
    dot_general x1, matrix products, on_device(): jnp.einsum('liw,lwr->lir', own_grads, right_factor.astype(jnp.bfloat16),...  9.56 us
    dot_general x1, matrix products, on_device(): jnp.einsum('liw,lir->lwr', own_grads, small_left, preferred_element_type=...  8.11 us
    dot_general x1, matrix products, on_device(): jnp.einsum('lir,lrw->liw', left, mixed, precision=lax.Precision.HIGHEST)  7.16 us
  transfers between devices with their start and end apart: 2, of which 2 were waited for; matrix products, arithmetic and copies ran while one was open for 4% of the time, Pallas kernels for 0%

commit v1 on v0

--- a/solution.py
+++ b/solution.py
@@ -4,6 +4,16 @@
 from jax.sharding import PartitionSpec as P
 
 RANK = 32
+
+
+def carry_the_spots(values, which_axis="dp"):
+    degree = lax.axis_size(which_axis)
+    lower, later = (values, 0)
+    while 1 << later < degree:
+        big = lax.ppermute(lower, which_axis, [(m, m ^ 1 << later) for m in range(degree)])
+        lower = lower + big
+        later = later + 1
+    return lower
 
 
 def on_device(gradients, right_factor, weights_before, momentum):
@@ -14,7 +24,7 @@
         right_factor.astype(jnp.bfloat16),
         preferred_element_type=jnp.float32,
     )
-    left = lax.psum(part_left, "dp")
+    left = carry_the_spots(part_left)
     part_gram = jnp.einsum("lir,lis->lrs", left, left, precision=lax.Precision.HIGHEST)
     small_left = left.astype(jnp.bfloat16)
     gram = lax.psum(part_gram, "tp")

time: 276 us -> 261 us (0.946)
  waiting for transfers between devices: 196 us -> 177 us
  starting transfers between devices: 0.08 us -> 7.54 us
    psum x1 -> x0, waiting for transfers between devices: 76.5 us -> none  [on_device(): left = lax.psum(part_left, 'dp')]
    ppermute x0 -> x3, waiting for transfers between devices: none -> 56.1 us  [carry_the_spots(): lax.ppermute(lower, which_axis, [(m, m ^ 1 << later) for m in range(degre...]
    ppermute x0 -> x3, starting transfers between devices: none -> 7.51 us  [carry_the_spots(): lax.ppermute(lower, which_axis, [(m, m ^ 1 << later) for m in range(degre...]
  transfers between devices with their start and end apart: 2 -> 4, of which waited for: 2 -> 4; matrix products, arithmetic and copies ran while one was open for 4% -> 4% of each run, Pallas kernels for 0% -> 0%
where the time goes in v1:
time: 261 us
  waiting for transfers between devices  177 us (68%)
  matrix products  26 us (10%)
  other arithmetic  24.4 us (9%)
  between operations  14.1 us (5%)
  blocking collectives  10.7 us (4%)
  starting transfers between devices  7.54 us (3%)
    psum x1, waiting for transfers between devices, on_device(): right = lax.psum(part_right, ('dp', 'tp'))  121 us
    ppermute x3, waiting for transfers between devices, carry_the_spots(): lax.ppermute(lower, which_axis, [(m, m ^ 1 << later) for m in range(degre...  56.1 us
    another operation x4, other arithmetic, on_device(): root = jnp.linalg.cholesky(gram)  11.9 us
    psum x1, blocking collectives, on_device(): gram = lax.psum(part_gram, 'tp')  10.7 us
    another operation x3, other arithmetic, on_device(): lax.linalg.triangular_solve(root, half, left_side=True, lower=True, trans...  9.93 us
    dot_general x1, matrix products, on_device(): jnp.einsum('liw,lwr->lir', own_grads, right_factor.astype(jnp.bfloat16),...  8.69 us
    dot_general x1, matrix products, on_device(): jnp.einsum('liw,lir->lwr', own_grads, small_left, preferred_element_type=...  7.88 us
    ppermute x3, starting transfers between devices, carry_the_spots(): lax.ppermute(lower, which_axis, [(m, m ^ 1 << later) for m in range(degre...  7.51 us
  transfers between devices with their start and end apart: 4, of which 4 were waited for; matrix products, arithmetic and copies ran while one was open for 4% of the time, Pallas kernels for 0%

profile of v1, /device:TPU:0, one launch (start us, length us, event | category | flops | bytes accessed | tf_op | source)
XLA Modules:
  0.0 261.2 jit_solution(13702040792497572471)
XLA Ops:
  7.2 0.0 all-reduce.2.cloned.1.call-start
  7.2 8.7 %fusion.2 = f32[4,1280,32]{1,2,0:T(8,128)S(1)} fusion(bf16[1,4,1280,1280]{3,2,1,0:T(8,128)(2,1)} %param.4, f32[4,1280,32]{1,2,0:T(8,128)} %param.5), kind=kOutput, calls=%fused_computation.3 | convolution fusion | flops 419594240 | bytes 14417920 | tf_op jit(solution)/shard_map/liw,lwr->lir/dot_general | solution.py:21
  15.9 3.0 %collective-permute-start = (f32[4,1280,32]{1,2,0:T(8,128)S(1)}, f32[4,1280,32]{1,2,0:T(8,128)S(1)}, u32[]{:S(2)}, u32[]{:S(2)}) collective-permute-start(f32[4,1280,32]{1,2,0:T(8,128)S(1)} %fusion.2), channel_id=1, source_target_pairs={{0,4},{4,0},{8,12},{12,8},{16,20},{20,16},{24,28},{28,24},{1,5},{5... | collective-permute-start | bytes 1966088 | tf_op jit(solution)/shard_map/ppermute | solution.py:13
  18.9 14.7 %collective-permute-done = f32[4,1280,32]{1,2,0:T(8,128)S(1)} collective-permute-done((f32[4,1280,32]{1,2,0:T(8,128)S(1)}, f32[4,1280,32]{1,2,0:T(8,128)S(1)}, u32[]{:S(2)}, u32[]{:S(2)}) %collective-permute-start) | collective-permute-done | bytes 655392 | tf_op jit(solution)/shard_map/ppermute | solution.py:13
  33.6 0.1 add.47
  33.7 1.9 collective-permute-start.1
  35.6 14.1 %collective-permute-done.1 = f32[4,1280,32]{1,2,0:T(8,128)S(1)} collective-permute-done((f32[4,1280,32]{1,2,0:T(8,128)S(1)}, f32[4,1280,32]{1,2,0:T(8,128)S(1)}, u32[]{:S(2)}, u32[]{:S(2)}) %collective-permute-start.1) | collective-permute-done | bytes 655392 | tf_op jit(solution)/shard_map/ppermute | solution.py:13
  49.7 0.1 add.48
  49.7 2.6 %collective-permute-start.2 = (f32[4,1280,32]{1,2,0:T(8,128)S(1)}, f32[4,1280,32]{1,2,0:T(8,128)S(1)}, u32[]{:S(2)}, u32[]{:S(2)}) collective-permute-start(f32[4,1280,32]{1,2,0:T(8,128)S(1)} %add.48), channel_id=1, source_target_pairs={{0,16},{4,20},{8,24},{12,28},{16,0},{20,4},{24,8},{28,12},{1,17},{... | collective-permute-start | bytes 1966088 | tf_op jit(solution)/shard_map/ppermute | solution.py:13
  52.4 0.1 copy.13
  52.5 27.3 %collective-permute-done.2 = f32[4,1280,32]{1,2,0:T(8,128)S(1)} collective-permute-done((f32[4,1280,32]{1,2,0:T(8,128)S(1)}, f32[4,1280,32]{1,2,0:T(8,128)S(1)}, u32[]{:S(2)}, u32[]{:S(2)}) %collective-permute-start.2) | collective-permute-done | bytes 655392 | tf_op jit(solution)/shard_map/ppermute | solution.py:13
  79.8 0.1 add.49
  79.9 0.7 fusion.18
  80.5 7.9 %fusion.5 = f32[4,1280,32]{1,2,0:T(8,128)} fusion(bf16[1,4,1280,1280]{3,2,1,0:T(8,128)(2,1)} %param.4, f32[4,1280,32]{1,2,0:T(8,128)S(1)} %add.49), kind=kOutput, calls=%fused_computation.8 | convolution fusion | flops 419594240 | bytes 14417920 | tf_op jit(solution)/shard_map/liw,lir->lwr/dot_general | solution.py:31
  88.4 10.7 %psum.14 = f32[4,32,32]{1,2,0:T(8,128)S(1)} all-reduce(f32[4,32,32]{1,2,0:T(8,128)S(1)} %fusion.18), channel_id=1, replica_groups=mesh['dp'=8,'tp'=4] {'tp'}, use_global_device_ids=true, to_apply=%region_0.0 | all-reduce | flops 4096 | bytes 32768 | tf_op jit(solution)/shard_map/psum | solution.py:30
  99.1 0.5 copy.12
  99.6 0.7 gather_fusion
  100.4 0.1 multiply_add_fusion
  100.4 0.1 copy.14
  100.5 0.1 fusion.15
  100.6 11.7 %custom-call.9 = f32[4,32,32]{2,1,0:T(8,128)S(1)} custom-call(f32[4,32,32]{2,1,0:T(8,128)S(1)} %fusion.15), custom_call_target="Cholesky" | custom-call | tf_op jit(solution)/shard_map/jit(cholesky)/cholesky | solution.py:40
  112.4 0.0 all-reduce.2.cloned.1.call-update
  112.4 0.1 compare_reduce_fusion
  112.5 0.1 select_bitcast_fusion
  112.6 9.8 %custom-call.10 = f32[4,1,32,32]{2,3,1,0:T(8,128)S(1)} custom-call(f32[4,1,32,32]{3,2,1,0:T(8,128)S(1)} %select_bitcast_fusion), custom_call_target="InvertDiagBlocksLowerTriangular" | custom-call | tf_op jit(solution)/shard_map/triangular_solve | solution.py:44
  122.5 120.9 %all-reduce.2.cloned.1.call-done = f32[4,1280,32]{1,2,0:T(8,128)} async-done(((f32[4,1280,32]{1,2,0:T(8,128)}), f32[4,1280,32]{1,2,0:T(8,128)}) %all-reduce.2.cloned.1.call-update) | async-done | bytes 655376 | tf_op jit(solution)/shard_map/psum | solution.py:34
  243.4 1.2 multiply_reduce_fusion
  244.6 1.3 fusion.10
  245.9 0.3 fusion.12
  246.2 0.0 copy-start
  246.2 7.2 %multiply_subtract_fusion = (f32[4,1280,160]{1,2,0:T(8,128)}, f32[4,1280,160]{1,2,0:T(8,128)}) fusion(f32[4,1280,160]{1,2,0:T(8,128)} %param.6, f32[4,1280,32]{1,2,0:T(8,128)S(1)} %add.49, f32[4,32,160]{2,1,0:T(8,128)S(1)} %fusion.12, f32[4,1280,160]{1,2,0:T(8,128)} %param.7), kind=kOutput, calls=%fused_computation.7 | convolution fusion | flops 318668800 | bytes 13844480 | tf_op jit(solution)/shard_map/lir,lrw->liw/dot_general | solution.py:45
  253.4 0.0 copy-done
  253.4 0.9 broadcast_multiply_fusion
  (8 shorter events, 0.1 us)
Async XLA Ops:
  7.2 236.2 %all-reduce.2.cloned.1.call-start = ((), (), s32[]{:S(2)}) async-start(), calls=%async_computation | async-start | bytes 1310720 | tf_op jit(solution)/shard_map/psum | solution.py:34
  15.9 17.7 %collective-permute-start = (f32[4,1280,32]{1,2,0:T(8,128)S(1)}, f32[4,1280,32]{1,2,0:T(8,128)S(1)}, u32[]{:S(2)}, u32[]{:S(2)}) collective-permute-start(f32[4,1280,32]{1,2,0:T(8,128)S(1)} %fusion.2), channel_id=1, source_target_pairs={{0,4},{4,0},{8,12},{12,8},{16,20},{20,16},{24,28},{28,24},{1,5},{5... | collective-permute-start | bytes 1966088 | tf_op jit(solution)/shard_map/ppermute | solution.py:13
  33.7 16.0 %collective-permute-start.1 = (f32[4,1280,32]{1,2,0:T(8,128)S(1)}, f32[4,1280,32]{1,2,0:T(8,128)S(1)}, u32[]{:S(2)}, u32[]{:S(2)}) collective-permute-start(f32[4,1280,32]{1,2,0:T(8,128)S(1)} %add.47), channel_id=1, source_target_pairs={{0,8},{4,12},{8,0},{12,4},{16,24},{20,28},{24,16},{28,20},{1,9},{5... | collective-permute-start | bytes 1966088 | tf_op jit(solution)/shard_map/ppermute | solution.py:13
  49.7 30.0 %collective-permute-start.2 = (f32[4,1280,32]{1,2,0:T(8,128)S(1)}, f32[4,1280,32]{1,2,0:T(8,128)S(1)}, u32[]{:S(2)}, u32[]{:S(2)}) collective-permute-start(f32[4,1280,32]{1,2,0:T(8,128)S(1)} %add.48), channel_id=1, source_target_pairs={{0,16},{4,20},{8,24},{12,28},{16,0},{20,4},{24,8},{28,12},{1,17},{... | collective-permute-start | bytes 1966088 | tf_op jit(solution)/shard_map/ppermute | solution.py:13
  246.2 7.2 %copy-start = (f32[4,1280,32]{1,2,0:T(8,128)S(1)}, f32[4,1280,32]{1,2,0:T(8,128)}, u32[]{:S(2)}) copy-start(f32[4,1280,32]{1,2,0:T(8,128)} %all-reduce.2.cloned.1.call-done) | copy-start | bytes 1966084
Sparse Core Ops, SparseCore 0:
  112.5 130.8 all-reduce.1
